TPU v7x, 256 devices: a whole 4x4x8 slice. The times are simulated.
256 devices in a mesh: dp: 16 (over y, x_hi, core), mp: 16 (over z, x_lo).
Axes of the slice: x: 4 (x_hi: 2, x_lo: 2; x = x_hi * 2 + x_lo), y: 4, z: 8, core: 2. Of those that a mesh axis runs over, the one named last changes fastest.
Arguments:
- grad_parts: bfloat16 [16, 1, 6144, 6144], P('dp', None, None, 'mp'), may hold values from -6 to 6
- master: float32 [1, 6144, 6144], P(None, 'dp', 'mp'), may hold values from -6 to 6
- momentum: float32 [1, 6144, 6144], P(None, 'dp', 'mp'), may hold values from -4 to 4
Outputs:
- new_master: float32 [1, 6144, 6144], P(None, 'dp', 'mp')
- new_momentum: float32 [1, 6144, 6144], P(None, 'dp', 'mp')
- new_weights: bfloat16 [1, 6144, 6144], P(None, None, 'mp')
All inputs are finite; a program needn't handle non-finite values.
Results may differ from a plain program's by a relative error of at most 0.0014.
Values may be sent and summed in bfloat16 or wider, within the bound.
A program may use at most 64 MiB of HBM per device.

v0:
```python
import jax
import jax.numpy as jnp
from jax import lax
from jax.sharding import PartitionSpec as P

beta_one = 0.9
beta_two = 0.99
step_size = 0.1
decay_rate = 0.1
softness = 0.05


def split_up(shard, dim, peers):
    lengths = shard.shape
    pieces = shard.reshape(*lengths[:dim], peers, lengths[dim] // peers, *lengths[dim + 1 :])
    return jnp.moveaxis(pieces, dim, 0)


def edges_of(length, count):
    turn = length // count
    if turn >= 8:
        turn -= turn % 8
    return [turn * k for k in range(1, count)]


def in_order(pieces, dim):
    lengths = list(pieces.shape[1:])
    lengths[dim] *= pieces.shape[0]
    return jnp.moveaxis(pieces, 0, dim).reshape(lengths)


def exchange_in_pieces(shard, axis, pieces, split_dim, concat_dim):
    blocks = split_up(shard, split_dim, lax.axis_size(axis))
    split_at = max(range(1, max(2, blocks.ndim - 1)), key=lambda d: blocks.shape[d])
    gathered = []
    for section in jnp.split(blocks, edges_of(blocks.shape[split_at], pieces), axis=split_at):
        if section.size:
            gathered.append(lax.all_to_all(section, axis, split_axis=0, concat_axis=0, tiled=True))
    return in_order(jnp.concatenate(gathered, axis=split_at), concat_dim)


def lion_update(gradient, master, momentum):
    interp = beta_one * momentum + (1.0 - beta_one) * gradient
    direction = interp / jnp.sqrt(interp * interp + softness * softness)
    new_master = master - step_size * (direction + decay_rate * master)
    new_momentum = beta_two * momentum + (1.0 - beta_two) * gradient
    return (new_master, new_momentum)


def per_device(grad_parts, master, momentum):
    replicas = lax.axis_size("dp")
    received = exchange_in_pieces(grad_parts, "dp", 2, 2, 0)
    summed = jnp.sum(received.astype(jnp.float32), axis=0)
    gradient = summed / replicas
    new_master, new_momentum = lion_update(gradient, master, momentum)
    new_weights = lax.all_gather(new_master.astype(jnp.bfloat16), "dp", axis=1, tiled=True)
    return (new_master, new_momentum, new_weights)


def solution(mesh):
    return jax.shard_map(
        per_device,
        mesh=mesh,
        in_specs=(P("dp", None, None, "mp"), P(None, "dp", "mp"), P(None, "dp", "mp")),
        out_specs=(P(None, "dp", "mp"), P(None, "dp", "mp"), P(None, None, "mp")),
        check_vma=False,
    )
```

profile of v0, /device:TPU:1, one launch (start us, length us, event | category | flops | bytes accessed | tf_op | source)
XLA Modules:
  0.0 159.1 jit_solution(11021761463291362914)
XLA Ops:
  7.2 0.0 all-gather.2.cloned.1.call-start
  7.2 2.9 %fusion.1 = (bf16[16,1,1,192,384]{4,3,2,1,0:T(8,128)(2,1)S(1)}, bf16[16,1,1,192,384]{4,3,2,1,0:T(8,128)(2,1)S(1)}) fusion(bf16[16,1,1,384,384]{4,3,2,1,0:T(8,128)(2,1)} %bitcast.8), kind=kLoop, calls=%fused_computation.5 | loop fusion | bytes 9437184 | tf_op jit(solution)/shard_map/split | solution.py:36
  10.1 39.4 %all_to_all.10 = bf16[16,1,1,192,384]{4,3,2,1,0:T(8,128)(2,1)S(1)} all-to-all(bf16[16,1,1,192,384]{4,3,2,1,0:T(8,128)(2,1)S(1)} %get-tuple-element.5), channel_id=1, replica_groups=mesh['dp'=16,'mp'=16] {'dp'}, dimensions={0} | all-to-all | bytes 4718592 | tf_op jit(solution)/shard_map/all_to_all | solution.py:38
  49.5 0.0 copy-start
  49.5 0.0 copy-start.1
  49.5 34.7 %all_to_all.11 = bf16[16,1,1,192,384]{4,3,2,1,0:T(8,128)(2,1)S(1)} all-to-all(bf16[16,1,1,192,384]{4,3,2,1,0:T(8,128)(2,1)S(1)} %get-tuple-element.6), channel_id=1, replica_groups=mesh['dp'=16,'mp'=16] {'dp'}, dimensions={0} | all-to-all | bytes 4718592 | tf_op jit(solution)/shard_map/all_to_all | solution.py:38
  84.2 0.6 convert_reduce_fusion
  84.8 0.0 copy-done
  84.8 0.0 copy-done.1
  84.9 1.3 fusion
  86.2 0.0 all-gather.2.cloned.1.call-update
  86.2 61.1 %all-gather.2.cloned.1.call-done = bf16[1,6144,384]{2,1,0:T(8,128)(2,1)} async-done(((bf16[1,384,384]{2,1,0:T(8,128)(2,1)}), bf16[1,6144,384]{2,1,0:T(8,128)(2,1)}) %all-gather.2.cloned.1.call-update) | async-done | bytes 4718608 | tf_op jit(solution)/shard_map/all_gather | solution.py:56
  147.3 5.0 %copy.7 = bf16[1,6144,384]{2,1,0:T(8,128)(2,1)} copy(bf16[1,6144,384]{2,1,0:T(8,128)(2,1)} %all-gather.2.cloned.1.call-done) | data formatting | bytes 9437184
Async XLA Ops:
  7.2 140.1 %all-gather.2.cloned.1.call-start = ((), (), s32[]{:S(2)}) async-start(), calls=%async_computation.2 | async-start | bytes 5013504 | tf_op jit(solution)/shard_map/all_gather | solution.py:56
  49.5 35.4 %copy-start = (f32[1,384,384]{2,1,0:T(8,128)S(1)}, f32[1,384,384]{2,1,0:T(8,128)}, u32[]{:S(2)}) copy-start(f32[1,384,384]{2,1,0:T(8,128)} %param.4) | copy-start | bytes 1769476
  49.5 35.4 %copy-start.1 = (f32[1,384,384]{2,1,0:T(8,128)S(1)}, f32[1,384,384]{2,1,0:T(8,128)}, u32[]{:S(2)}) copy-start(f32[1,384,384]{2,1,0:T(8,128)} %param.5) | copy-start | bytes 1769476
Sparse Core Ops, SparseCore 0:
  86.4 60.8 all-gather.1
where the time goes:
time: 159 us
  blocking collectives  74.1 us (47%)
  waiting for transfers between devices  61.1 us (38%)
  between operations  14.1 us (9%)
  local copies, waits for them, and re-layouts  7.86 us (5%)
  other arithmetic  2 us (1%)
    all_to_all x2, blocking collectives, exchange_in_pieces(): lax.all_to_all(section, axis, split_axis=0, concat_axis=0, tiled=True)  74.1 us
    all_gather x1, waiting for transfers between devices, per_device(): lax.all_gather(new_master.astype(jnp.bfloat16), 'dp', axis=1, tiled=True)  61.1 us
    unnamed x5, local copies, waits for them, and re-layouts  5 us
  transfers between devices with their start and end apart: 1, of which 1 were waited for; matrix products, arithmetic and copies ran while one was open for 0% of the time, Pallas kernels for 0%

commit v1 on v0

v1 whole, which is shorter than its diff:
```python
import functools

import jax
import jax.numpy as jnp
from jax import lax
from jax.experimental import pallas as pl
from jax.experimental.pallas import tpu as pltpu
from jax.sharding import PartitionSpec as P

beta_one = 0.9
beta_two = 0.99
step_size = 0.1
decay_rate = 0.1
softness = 0.05

MESH = pl.DeviceIdType.MESH
A, B, X = 4, 2, 1

PIECES = ((0, 96, (A, X, B), (B, X, A)), (96, 96, (A, X, B), (B, X, A)), (192, 96, (A, X, B), (B, X, A)), (288, 96, (A, X, B), (B, X, A)))
LAG = 3.2


def reduce_slots(order, stage):
    taken = sum(order[:stage])
    slots = [s for s in range(8) if s & order[stage] and not s & taken]
    later = order[stage + 1 :]

    def urgency(s):
        hit = [i for i, d in enumerate(later) if s & d]
        return hit[0] if hit else len(later)

    return sorted(slots, key=urgency)


def tasks_of(piece, number):
    first, rows, down, up = piece
    start = number * LAG
    out = []
    for stage, at in ((0, 0.0), (1, 5.0), (2, 10.5)):
        for k, s in enumerate(reduce_slots(down, stage)):
            out.append((start + at + 0.2 * k, number, "reduce", stage, s))
    out.append((start + 13.5, number, "update", 0, 0))
    e1, e2, e3 = up
    for at, s in ((16.0, e1), (18.0, e2), (20.0, e1 + e2), (17.0, e3), (19.0, e1 + e3), (21.0, e2 + e3), (23.0, e1 + e2 + e3)):
        out.append((start + at, number, "spread", 0, s))
    return out


def kernel(
    grad, master, momentum, new_master, new_momentum, weights,
    own, part, outgoing, incoming, master_in, momentum_in,
    load_sem, pair_send, pair_recv, down_send, down_recv, up_send, up_recv, twin_send, twin_recv,
):
    dp, mp = lax.axis_index("dp"), lax.axis_index("mp")
    core, xh, y = lax.rem(dp, 2), lax.rem(dp // 2, 2), dp // 4
    side = 1 - 2 * lax.rem(y + core, 2)

    def device(y_at, x_at, c_at):
        return ((y_at * 2 + x_at) * 2 + c_at, mp)

    y_of = (y, lax.rem(y + 4 - side, 4), lax.rem(y + 4 + side, 4), lax.rem(y + 2, 4))
    x_of = (xh, 1 - xh)
    twin = device(y, xh, 1 - core)
    peer = {A: device(y_of[2], xh, core), B: device(y_of[1], xh, core), X: device(y, 1 - xh, core)}

    def tile_of(slot):
        return y_of[slot // 2], x_of[slot % 2]

    loads = [
        pltpu.make_async_copy(grad.at[:, :, core], own, load_sem.at[0]),
        pltpu.make_async_copy(master, master_in, load_sem.at[1]),
        pltpu.make_async_copy(momentum, momentum_in, load_sem.at[2]),
    ]
    for load in loads:
        load.start()

    barrier = pltpu.get_barrier_semaphore()
    for other in (twin, peer[A], peer[B], peer[X]):
        pl.semaphore_signal(barrier, inc=1, device_id=other, device_id_type=MESH)
    pl.semaphore_wait(barrier, 4)

    pairs = []
    for n, (first, rows, _, _) in enumerate(PIECES):
        at = pl.ds(first, rows)
        pairs.append(
            pltpu.make_async_remote_copy(
                src_ref=grad.at[:, :, 1 - core, at],
                dst_ref=part.at[:, :, at],
                send_sem=pair_send,
                recv_sem=pair_recv.at[n],
                device_id=twin,
                device_id_type=MESH,
            )
        )
        pairs[-1].start()
    loads[0].wait()

    def down_copy(n, slot, d):
        at = pl.ds(PIECES[n][0], PIECES[n][1])
        return pltpu.make_async_remote_copy(
            src_ref=outgoing.at[slot - 1, at],
            dst_ref=incoming.at[slot - 1, at],
            send_sem=down_send,
            recv_sem=down_recv.at[n * 7 + slot - 1],
            device_id=peer[d],
            device_id_type=MESH,
        )

    def up_copy(n, slot, d):
        at = pl.ds(PIECES[n][0], PIECES[n][1])
        ty, tx = tile_of(slot)
        here = weights.at[ty, tx, core, at]
        return pltpu.make_async_remote_copy(
            src_ref=here,
            dst_ref=here,
            send_sem=up_send,
            recv_sem=up_recv.at[n * 7 + (slot ^ d) - 1],
            device_id=peer[d],
            device_id_type=MESH,
        )

    def twin_copy(n, slot):
        at = pl.ds(PIECES[n][0], PIECES[n][1])
        ty, tx = tile_of(slot)
        here = weights.at[ty, tx, core, at]
        return pltpu.make_async_remote_copy(
            src_ref=here,
            dst_ref=here,
            send_sem=twin_send,
            recv_sem=twin_recv,
            device_id=twin,
            device_id_type=MESH,
        )

    def summed(n, slot, sources):
        at = pl.ds(PIECES[n][0], PIECES[n][1])
        ty, tx = tile_of(slot)
        total = own[ty, tx, at].astype(jnp.float32) + part[ty, tx, at].astype(jnp.float32)
        for source in sources:
            total += incoming[source - 1, at].astype(jnp.float32)
        return total

    begun, pair_in = set(), set()
    for _, n, kind, stage, slot in sorted(t for i, p in enumerate(PIECES) for t in tasks_of(p, i)):
        first, rows, down, up = PIECES[n]
        at = pl.ds(first, rows)
        if n not in pair_in:
            pairs[n].wait_recv()
            pair_in.add(n)
        if kind == "reduce":
            for d in down[:stage]:
                down_copy(n, slot | d, d).wait_recv()
            outgoing[slot - 1, at] = summed(n, slot, [slot | d for d in down[:stage]]).astype(jnp.bfloat16)
            down_copy(n, slot, down[stage]).start()
        elif kind == "update":
            if not begun:
                loads[1].wait()
                loads[2].wait()
                begun.add(n)
            for d in down:
                down_copy(n, d, d).wait_recv()
            gradient = summed(n, 0, down) / 16
            old_master, old_momentum = master_in[at], momentum_in[at]
            interp = beta_one * old_momentum + (1.0 - beta_one) * gradient
            direction = interp * lax.rsqrt(interp * interp + softness * softness)
            fresh = old_master - step_size * (direction + decay_rate * old_master)
            weights[y, xh, core, at] = fresh.astype(jnp.bfloat16)
            for d in up:
                up_copy(n, 0, d).start()
            twin_copy(n, 0).start()
            new_master[at] = fresh
            new_momentum[at] = beta_two * old_momentum + (1.0 - beta_two) * gradient
        else:
            last = max(i for i, d in enumerate(up) if slot & d)
            up_copy(n, slot ^ up[last], up[last]).wait_recv()
            for d in up[last + 1 :]:
                up_copy(n, slot, d).start()
            twin_copy(n, slot).start()

    pltpu.make_async_copy(own, own, twin_recv).wait()
    pltpu.make_async_copy(own, own, twin_send).wait()
    pltpu.make_async_copy(own, own, pair_send).wait()
    pltpu.make_async_copy(outgoing, outgoing, down_send).wait()
    pltpu.make_async_copy(outgoing, outgoing, up_send).wait()


def per_device(grad_parts, master, momentum):
    side, columns = master.shape[1:]
    grad = grad_parts.reshape(4, 2, 2, side, columns)
    pieces = len(PIECES)
    new_master, new_momentum, weights = pl.pallas_call(
        kernel,
        out_shape=(
            jax.ShapeDtypeStruct((side, columns), jnp.float32),
            jax.ShapeDtypeStruct((side, columns), jnp.float32),
            jax.ShapeDtypeStruct((4, 2, 2, side, columns), jnp.bfloat16),
        ),
        in_specs=[pl.BlockSpec(memory_space=pl.ANY)] * 3,
        out_specs=[pl.BlockSpec(memory_space=pltpu.VMEM)] * 3,
        scratch_shapes=[
            pltpu.VMEM((4, 2, side, columns), jnp.bfloat16),
            pltpu.VMEM((4, 2, side, columns), jnp.bfloat16),
            pltpu.VMEM((7, side, columns), jnp.bfloat16),
            pltpu.VMEM((7, side, columns), jnp.bfloat16),
            pltpu.VMEM((side, columns), jnp.float32),
            pltpu.VMEM((side, columns), jnp.float32),
            pltpu.SemaphoreType.DMA((3,)),
            pltpu.SemaphoreType.DMA,
            pltpu.SemaphoreType.DMA((pieces,)),
            pltpu.SemaphoreType.DMA,
            pltpu.SemaphoreType.DMA((7 * pieces,)),
            pltpu.SemaphoreType.DMA,
            pltpu.SemaphoreType.DMA((7 * pieces,)),
            pltpu.SemaphoreType.DMA,
            pltpu.SemaphoreType.DMA,
        ],
        compiler_params=pltpu.CompilerParams(collective_id=0, has_side_effects=True, vmem_limit_bytes=48 * 2**20),
    )(grad, master.reshape(side, columns), momentum.reshape(side, columns))
    return (
        new_master.reshape(1, side, columns),
        new_momentum.reshape(1, side, columns),
        weights.reshape(1, 16 * side, columns),
    )


def solution(mesh):
    return jax.shard_map(
        per_device,
        mesh=mesh,
        in_specs=(P("dp", None, None, "mp"), P(None, "dp", "mp"), P(None, "dp", "mp")),
        out_specs=(P(None, "dp", "mp"), P(None, "dp", "mp"), P(None, None, "mp")),
        check_vma=False,
    )
```

time: 159 us -> 63 us (0.40)
  blocking collectives: 74.1 us -> 0 us
  waiting for transfers between devices: 61.1 us -> 0 us
  Pallas kernels: 0 us -> 53.3 us
  between operations: 14.1 us -> 0.65 us
  other arithmetic: 2 us -> 0 us
    all_to_all x2 -> x0, blocking collectives: 74.1 us -> none  [exchange_in_pieces(): lax.all_to_all(section, axis, split_axis=0, concat_axis=0, tiled=True)]
    all_gather x1 -> x0, waiting for transfers between devices: 61.1 us -> none  [per_device(): lax.all_gather(new_master.astype(jnp.bfloat16), 'dp', axis=1, tiled=True)]
    pallas_call x0 -> x1, Pallas kernels: none -> 53.3 us  [per_device(): pl.pallas_call(kernel, out_shape=(jax.ShapeDtypeStruct((side, columns), j...]
    unnamed x5 -> x7, local copies, waits for them, and re-layouts: 5 us -> 8.75 us
    split x1 -> x0, local copies, waits for them, and re-layouts: 2.86 us -> none  [exchange_in_pieces(): jnp.split(blocks, edges_of(blocks.shape[split_at], pieces), axis=split_at)]
  transfers between devices with their start and end apart: 1 -> 0, of which waited for: 1 -> 0; matrix products, arithmetic and copies ran while one was open for 0% -> 0% of each run, Pallas kernels for 0% -> 0%
where the time goes in v1:
time: 63 us; the launch traced here: 62.7 us
  Pallas kernels  53.3 us (85%)
  local copies, waits for them, and re-layouts  8.75 us (14%)
  between operations  0.65 us (1%)
    pallas_call x1, Pallas kernels, per_device(): pl.pallas_call(kernel, out_shape=(jax.ShapeDtypeStruct((side, columns), j...  53.3 us
    unnamed x7, local copies, waits for them, and re-layouts  8.75 us

profile of v1, /device:TPU:1, one launch (start us, length us, event | category | flops | bytes accessed | tf_op | source)
XLA Modules:
  0.0 62.7 jit_solution(5692097463481388500)
XLA Ops:
  0.6 0.0 copy-start
  0.6 1.1 %copy-done = f32[1,384,384]{2,1,0:T(8,128)S(1)} copy-done((f32[1,384,384]{2,1,0:T(8,128)S(1)}, f32[1,384,384]{2,1,0:T(8,128)}, u32[]{:S(2)}) %copy-start) | copy-done | bytes 589848
  1.7 0.0 copy-start.1
  1.7 1.1 %copy-done.1 = f32[1,384,384]{2,1,0:T(8,128)S(1)} copy-done((f32[1,384,384]{2,1,0:T(8,128)S(1)}, f32[1,384,384]{2,1,0:T(8,128)}, u32[]{:S(2)}) %copy-start.1) | copy-done | bytes 589848
  2.8 53.3 %shard_map.58 = (f32[384,384]{1,0:T(8,128)S(1)}, f32[384,384]{1,0:T(8,128)S(1)}, bf16[4,2,2,384,384]{4,3,2,1,0:T(8,128)(2,1)}) custom-call(bf16[4,2,2,384,384]{4,3,2,1,0:T(8,128)(2,1)} %bitcast.10, f32[384,384]{1,0:T(8,128)S(1)} %bitcast.6, f32[384,384]{1,0:T(8,128)S(1)} %bitcast.7), custom_call_target="tpu_custom_call" | custom-call | tf_op jit(solution)/shard_map/pallas_call | solution.py:191
  56.1 0.8 %copy.9 = f32[1,384,384]{2,1,0:T(8,128)} copy(f32[1,384,384]{2,1,0:T(8,128)S(1)} %bitcast.9) | data formatting | bytes 1179648
  56.9 0.8 %copy.10 = f32[1,384,384]{2,1,0:T(8,128)} copy(f32[1,384,384]{2,1,0:T(8,128)S(1)} %bitcast.8) | data formatting | bytes 1179648
  57.7 5.0 %copy.11 = bf16[1,6144,384]{2,1,0:T(8,128)(2,1)} copy(bf16[1,6144,384]{2,1,0:T(8,128)(2,1)} %bitcast.11) | data formatting | bytes 9437184
Async XLA Ops:
  0.6 1.1 %copy-start = (f32[1,384,384]{2,1,0:T(8,128)S(1)}, f32[1,384,384]{2,1,0:T(8,128)}, u32[]{:S(2)}) copy-start(f32[1,384,384]{2,1,0:T(8,128)} %param.4) | copy-start | bytes 1769476
  1.7 1.1 %copy-start.1 = (f32[1,384,384]{2,1,0:T(8,128)S(1)}, f32[1,384,384]{2,1,0:T(8,128)}, u32[]{:S(2)}) copy-start(f32[1,384,384]{2,1,0:T(8,128)} %param.5) | copy-start | bytes 1769476

commit v2 on v1

--- a/solution.py
+++ b/solution.py
@@ -16,34 +16,24 @@
 MESH = pl.DeviceIdType.MESH
 A, B, X = 4, 2, 1
 
-PIECES = ((0, 96, (A, X, B), (B, X, A)), (96, 96, (A, X, B), (B, X, A)), (192, 96, (A, X, B), (B, X, A)), (288, 96, (A, X, B), (B, X, A)))
-LAG = 3.2
-
-
-def reduce_slots(order, stage):
-    taken = sum(order[:stage])
-    slots = [s for s in range(8) if s & order[stage] and not s & taken]
-    later = order[stage + 1 :]
-
-    def urgency(s):
-        hit = [i for i, d in enumerate(later) if s & d]
-        return hit[0] if hit else len(later)
-
-    return sorted(slots, key=urgency)
-
-
-def tasks_of(piece, number):
-    first, rows, down, up = piece
-    start = number * LAG
-    out = []
-    for stage, at in ((0, 0.0), (1, 5.0), (2, 10.5)):
-        for k, s in enumerate(reduce_slots(down, stage)):
-            out.append((start + at + 0.2 * k, number, "reduce", stage, s))
-    out.append((start + 13.5, number, "update", 0, 0))
-    e1, e2, e3 = up
-    for at, s in ((16.0, e1), (18.0, e2), (20.0, e1 + e2), (17.0, e3), (19.0, e1 + e3), (21.0, e2 + e3), (23.0, e1 + e2 + e3)):
-        out.append((start + at, number, "spread", 0, s))
-    return out
+PIECES = (
+    (0, 16, (A, B, X), (B, A, X)),
+    (16, 32, (X, B, A), (A, B, X)),
+    (48, 32, (B, A, X), (B, X, A)),
+    (80, 64, (B, A, X), (X, B, A)),
+    (144, 80, (X, A, B), (A, B, X)),
+    (224, 48, (B, A, X), (B, X, A)),
+    (272, 64, (B, A, X), (X, B, A)),
+    (336, 48, (X, A, B), (X, B, A)),
+)
+STEPS = (
+    6, 7, 5, 4, 19, 23, 21, 17, 38, 39, 35, 34, 54, 55, 51, 50, 69, 71, 67, 65,
+    86, 87, 83, 82, 102, 103, 99, 98, 2, 3, 117, 119, 115, 113, 36, 37, 18, 22, 52, 53,
+    68, 84, 33, 85, 70, 49, 100, 101, 116, 118, 81, 66, 1, 40, 20, 97, 56, 114, 88, 72,
+    44, 8, 42, 24, 41, 60, 58, 104, 92, 120, 57, 90, 76, 89, 12, 46, 74, 10, 28, 73,
+    9, 26, 45, 43, 25, 106, 62, 122, 105, 108, 121, 59, 124, 91, 61, 78, 94, 30, 77, 93,
+    13, 14, 47, 107, 75, 110, 11, 123, 126, 29, 109, 27, 125, 63, 95, 79, 111, 31, 127, 15,
+)
 
 
 def kernel(
@@ -140,23 +130,31 @@
             total += incoming[source - 1, at].astype(jnp.float32)
         return total
 
-    begun, pair_in = set(), set()
-    for _, n, kind, stage, slot in sorted(t for i, p in enumerate(PIECES) for t in tasks_of(p, i)):
+    ready, paired = False, set()
+    for step in STEPS:
+        n, slot = step // 16, step % 8
         first, rows, down, up = PIECES[n]
         at = pl.ds(first, rows)
-        if n not in pair_in:
+        if n not in paired:
             pairs[n].wait_recv()
-            pair_in.add(n)
-        if kind == "reduce":
+            paired.add(n)
+        if step % 16 >= 8 and slot:
+            last = max(i for i, d in enumerate(up) if slot & d)
+            up_copy(n, slot ^ up[last], up[last]).wait_recv()
+            for d in up[last + 1 :]:
+                up_copy(n, slot, d).start()
+            twin_copy(n, slot).start()
+        elif slot:
+            stage = min(i for i, d in enumerate(down) if slot & d)
             for d in down[:stage]:
                 down_copy(n, slot | d, d).wait_recv()
             outgoing[slot - 1, at] = summed(n, slot, [slot | d for d in down[:stage]]).astype(jnp.bfloat16)
             down_copy(n, slot, down[stage]).start()
-        elif kind == "update":
-            if not begun:
+        else:
+            if not ready:
                 loads[1].wait()
                 loads[2].wait()
-                begun.add(n)
+                ready = True
             for d in down:
                 down_copy(n, d, d).wait_recv()
             gradient = summed(n, 0, down) / 16
@@ -170,12 +168,6 @@
             twin_copy(n, 0).start()
             new_master[at] = fresh
             new_momentum[at] = beta_two * old_momentum + (1.0 - beta_two) * gradient
-        else:
-            last = max(i for i, d in enumerate(up) if slot & d)
-            up_copy(n, slot ^ up[last], up[last]).wait_recv()
-            for d in up[last + 1 :]:
-                up_copy(n, slot, d).start()
-            twin_copy(n, slot).start()
 
     pltpu.make_async_copy(own, own, twin_recv).wait()
     pltpu.make_async_copy(own, own, twin_send).wait()
@@ -184,18 +176,28 @@
     pltpu.make_async_copy(outgoing, outgoing, up_send).wait()
 
 
+def put_out(fresh, moved, rounded, new_master, new_momentum, weights, sem):
+    copies = [
+        pltpu.make_async_copy(fresh, new_master, sem.at[0]),
+        pltpu.make_async_copy(moved, new_momentum, sem.at[1]),
+    ]
+    for n in range(4):
+        copies.append(pltpu.make_async_copy(rounded.at[n], weights.at[n], sem.at[2 + n]))
+    for copy in copies:
+        copy.start()
+    for copy in copies:
+        copy.wait()
+
+
 def per_device(grad_parts, master, momentum):
     side, columns = master.shape[1:]
     grad = grad_parts.reshape(4, 2, 2, side, columns)
     pieces = len(PIECES)
-    new_master, new_momentum, weights = pl.pallas_call(
+    outs = (((side, columns), jnp.float32), ((side, columns), jnp.float32), ((4, 2, 2, side, columns), jnp.bfloat16))
+    results = pl.pallas_call(
         kernel,
-        out_shape=(
-            jax.ShapeDtypeStruct((side, columns), jnp.float32),
-            jax.ShapeDtypeStruct((side, columns), jnp.float32),
-            jax.ShapeDtypeStruct((4, 2, 2, side, columns), jnp.bfloat16),
-        ),
-        in_specs=[pl.BlockSpec(memory_space=pl.ANY)] * 3,
+        out_shape=[pltpu.VMEM(*o) for o in outs],
+        in_specs=[pl.BlockSpec(memory_space=pltpu.HBM)] * 3,
         out_specs=[pl.BlockSpec(memory_space=pltpu.VMEM)] * 3,
         scratch_shapes=[
             pltpu.VMEM((4, 2, side, columns), jnp.bfloat16),
@@ -216,6 +218,14 @@
         ],
         compiler_params=pltpu.CompilerParams(collective_id=0, has_side_effects=True, vmem_limit_bytes=48 * 2**20),
     )(grad, master.reshape(side, columns), momentum.reshape(side, columns))
+    new_master, new_momentum, weights = pl.pallas_call(
+        put_out,
+        out_shape=[jax.ShapeDtypeStruct(*o) for o in outs],
+        in_specs=[pl.BlockSpec(memory_space=pltpu.VMEM)] * 3,
+        out_specs=[pl.BlockSpec(memory_space=pltpu.HBM)] * 3,
+        scratch_shapes=[pltpu.SemaphoreType.DMA((6,))],
+        compiler_params=pltpu.CompilerParams(vmem_limit_bytes=2**20),
+    )(*[pltpu.with_memory_space_constraint(r, pltpu.VMEM) for r in results])
     return (
         new_master.reshape(1, side, columns),
         new_momentum.reshape(1, side, columns),

time: 63 us -> 45.4 us (0.72)
  local copies, waits for them, and re-layouts: 8.75 us -> 0 us
  Pallas kernels: 53.3 us -> 44.7 us
    unnamed x7 -> x0, local copies, waits for them, and re-layouts: 8.75 us -> none
    pallas_call x1 -> x2, Pallas kernels: 53.3 us -> 44.7 us  [the longest x1 42.1 us: per_device(): pl.pallas_call(kernel, out_shape=[pltpu.VMEM(*o) for o in outs], in_specs...]
where the time goes in v2:
time: 45.4 us
  Pallas kernels  44.7 us (98%)
  between operations  0.64 us (1%)
    pallas_call x1, Pallas kernels, per_device(): pl.pallas_call(kernel, out_shape=[pltpu.VMEM(*o) for o in outs], in_specs...  42.1 us
    pallas_call x1, Pallas kernels, per_device(): pl.pallas_call(put_out, out_shape=[jax.ShapeDtypeStruct(*o) for o in outs...  2.62 us

profile of v2, /device:TPU:1, one launch (start us, length us, event | category | flops | bytes accessed | tf_op | source)
XLA Modules:
  0.0 45.4 jit_solution(16290507010035676722)
XLA Ops:
  0.6 42.1 %shard_map.58 = (f32[384,384]{1,0:T(8,128)S(1)}, f32[384,384]{1,0:T(8,128)S(1)}, bf16[4,2,2,384,384]{4,3,2,1,0:T(8,128)(2,1)S(1)}) custom-call(bf16[4,2,2,384,384]{4,3,2,1,0:T(8,128)(2,1)} %bitcast.6, f32[384,384]{1,0:T(8,128)} %bitcast.7, f32[384,384]{1,0:T(8,128)} %bitcast.8), custom_call_target="tpu_custom_call" | custom-call | tf_op jit(solution)/shard_map/pallas_call | solution.py:197
  42.7 2.6 %shard_map.59 = (f32[384,384]{1,0:T(8,128)}, f32[384,384]{1,0:T(8,128)}, bf16[4,2,2,384,384]{4,3,2,1,0:T(8,128)(2,1)}) custom-call(f32[384,384]{1,0:T(8,128)S(1)} %get-tuple-element.9.fresh, f32[384,384]{1,0:T(8,128)S(1)} %get-tuple-element.10.moved, bf16[4,2,2,384,384]{4,3,2,1,0:T(8,128)(2,1)S(1)} %get-tuple-element.11.rounded), custom_call_target="tpu_custom_call" | custom-call | tf_op jit(solution)/shard_map/pallas_call | solution.py:221

commit v3 on v2

v3 whole, which is shorter than its diff:
```python
import functools

import jax
import jax.numpy as jnp
from jax import lax
from jax.experimental import pallas as pl
from jax.experimental.pallas import tpu as pltpu
from jax.sharding import PartitionSpec as P

beta_one = 0.9
beta_two = 0.99
step_size = 0.1
decay_rate = 0.1
softness = 0.05

MESH = pl.DeviceIdType.MESH
A, B, X = 4, 2, 1

PIECES = (
    (0, 32, (B, A, X), (A, X, B)),
    (32, 32, (X, A, B), (A, X, B)),
    (64, 32, (X, A, B), (X, A, B)),
    (96, 48, (A, X, B), (X, A, B)),
    (144, 64, (B, A, X), (B, A, X)),
    (208, 32, (B, A, X), (A, B, X)),
    (240, 48, (X, A, B), (B, A, X)),
    (288, 48, (X, B, A), (X, A, B)),
    (336, 48, (B, A, X), (X, A, B)),
)
EARLY = 64
STEPS = (
    7, 21, 23, 2, 3, 19, 71, 55, 103, 86, 52, 82, 135, 39, 67, 54, 134, 101, 87, 37,
    35, 119, 5, 99, 53, 69, 6, 33, 117, 51, 70, 131, 102, 115, 22, 133, 36, 1, 38, 84,
    65, 118, 83, 98, 66, 85, 130, 49, 113, 68, 129, 50, 4, 100, 81, 116, 20, 17, 114, 34,
    132, 18, 97, 72, 56, 8, 120, 24, 88, 136, 104, 12, 40, 121, 74, 25, 92, 28, 60, 57,
    106, 137, 108, 13, 94, 9, 140, 76, 124, 78, 41, 110, 75, 125, 30, 29, 141, 44, 61, 90,
    93, 45, 123, 127, 43, 59, 31, 14, 79, 15, 107, 139, 111, 63, 95, 143, 47,
)


def parse(step):
    n, slot = step // 16, step % 8
    return n, slot, "up" if step % 16 > 8 else "down"


def arrival_of(n, way, slot):
    up = PIECES[n][3]
    return (n, way, slot | up[0] if way == "up" and slot & up[2] else slot)


def stage_of(order, slot):
    return min((i for i, d in enumerate(order) if slot & d), default=3)


def tiles_of(n, slot):
    up = PIECES[n][3]
    return [slot ^ up[0], slot] if slot & up[2] else [slot]


def beyond(n, slot):
    up = PIECES[n][3]
    return up[max(i for i, d in enumerate(up) if slot & d) + 1 :]


def messages_of(step):
    n, slot, way = parse(step)
    down, up = PIECES[n][2:]
    if way == "up":
        return [(d, arrival_of(n, way, s | d)) for s in tiles_of(n, slot) for d in beyond(n, s)]
    if slot:
        d = down[stage_of(down, slot)]
        return [(d, (n, way, slot ^ d))]
    return [(d, arrival_of(n, "up", d)) for d in up]


def numbered():
    first, sent = {}, {}
    for at, step in enumerate(STEPS):
        n, slot, way = parse(step)
        halves = () if way == "up" else (0,) if stage_of(PIECES[n][2], slot) == 0 else (0, 1)
        for key in [(n, way, slot)] + [(n, "pair", half) for half in halves]:
            first.setdefault(key, at)
        for d, key in messages_of(step):
            sent.setdefault(key, []).append((d, at))
    links = [(d, at, first[key]) for key in sent for d, at in sent[key]]
    number, last = {}, []
    for n in range(len(PIECES)):
        for half in range(2):
            number[n, "pair", half] = len(last)
            last.append(first[n, "pair", half])
    for key in sorted(sent, key=lambda k: min(at for _, at in sent[k])):
        fit = [
            (then, i)
            for i, then in enumerate(last)
            if all(any(d == e and then <= v and r <= at for e, v, r in links) for d, at in sent[key])
        ]
        i = max(fit)[1] if fit else len(last)
        if not fit:
            last.append(0)
        number[key], last[i] = i, first[key]
    return number, len(last)


NUMBER, SEMAPHORES = numbered()


def kernel(
    grad, master, momentum, new_master, new_momentum, weights,
    own, other, part, outgoing, incoming, master_in, momentum_in,
    load_sem, recv_sem, pair_send, down_send, up_send, twin_send, twin_recv,
):
    dp, mp = lax.axis_index("dp"), lax.axis_index("mp")
    core, xh, y = lax.rem(dp, 2), lax.rem(dp // 2, 2), dp // 4
    side = 1 - 2 * lax.rem(y + core, 2)

    def device(y_at, x_at, c_at):
        return ((y_at * 2 + x_at) * 2 + c_at, mp)

    y_of = (y, lax.rem(y + 4 - side, 4), lax.rem(y + 4 + side, 4), lax.rem(y + 2, 4))
    x_of = (xh, 1 - xh)
    twin = device(y, xh, 1 - core)
    peer = {A: device(y_of[2], xh, core), B: device(y_of[1], xh, core), X: device(y, 1 - xh, core)}

    def tile_of(slot):
        return y_of[slot // 2], x_of[slot % 2]

    def rows_of(n):
        return pl.ds(PIECES[n][0], PIECES[n][1])

    def send(source, target, send_sem, recv_sem, to):
        pltpu.make_async_remote_copy(
            src_ref=source, dst_ref=target, send_sem=send_sem, recv_sem=recv_sem, device_id=to, device_id_type=MESH
        ).start()

    def await_bytes(ref, sem):
        pltpu.make_async_copy(ref, ref, sem).wait()

    barrier = pltpu.get_barrier_semaphore()
    for neighbour in (twin, peer[A], peer[B], peer[X]):
        pl.semaphore_signal(barrier, inc=1, device_id=neighbour, device_id_type=MESH)

    loads = []
    for start, stop in ((0, EARLY), (EARLY, own.shape[2])):
        at = pl.ds(start, stop - start)
        for of, to in ((1 - core, other), (core, own)):
            loads.append(pltpu.make_async_copy(grad.at[:, :, of, at], to.at[:, :, at], load_sem.at[len(loads)]))
    loads.append(pltpu.make_async_copy(master, master_in, load_sem.at[4]))
    loads.append(pltpu.make_async_copy(momentum, momentum_in, load_sem.at[5]))
    for load in loads:
        load.start()
    there = set()

    def need(key, wait):
        if key not in there:
            wait()
            there.add(key)

    pl.semaphore_wait(barrier, 4)

    for half in range(2):
        for n, (first, rows, down, _) in enumerate(PIECES):
            load = 0 if first < EARLY else 2
            need(("load", load), loads[load].wait)
            at = rows_of(n)
            if down[0] == X:
                spots = [(slice(None), x_of[1 - half])]
            elif down[0] == A:
                spots = [(y_of[k], slice(None)) for k in ((1, 3), (0, 2))[half]]
            else:
                spots = [(y_of[k], slice(None)) for k in ((2, 3), (0, 1))[half]]
            for ty, tx in spots:
                send(other.at[ty, tx, at], part.at[ty, tx, at], pair_send, recv_sem.at[NUMBER[n, "pair", half]], twin)

    def pass_up(n, slot, along):
        ty, tx = tile_of(slot)
        here = weights.at[ty, tx, core, rows_of(n)]
        for d in along:
            send(here, here, up_send, recv_sem.at[NUMBER[arrival_of(n, "up", slot | d)]], peer[d])
        send(here, here, twin_send, twin_recv, twin)

    def summed(n, slot, sources):
        at = rows_of(n)
        if sources:
            await_bytes(incoming.at[pl.ds(0, len(sources)), at], recv_sem.at[NUMBER[n, "down", slot]])
        ty, tx = tile_of(slot)
        total = own[ty, tx, at].astype(jnp.float32) + part[ty, tx, at].astype(jnp.float32)
        for source in sources:
            total += incoming[source - 1, at].astype(jnp.float32)
        return total

    for step in STEPS:
        n, slot, way = parse(step)
        first, rows, down, up = PIECES[n]
        at = rows_of(n)
        if way == "up":
            tiles = tiles_of(n, slot)
            await_bytes(incoming.at[pl.ds(0, len(tiles)), at], recv_sem.at[NUMBER[n, way, slot]])
            for tile in tiles:
                pass_up(n, tile, beyond(n, tile))
            continue
        load = 1 if first < EARLY else 3
        need(("load", load), loads[load].wait)
        stage = stage_of(down, slot)
        for half in range(2 if stage else 1):
            need(("part", n, half), lambda: await_bytes(part.at[:, 0, at], recv_sem.at[NUMBER[n, "pair", half]]))
        if slot:
            outgoing[slot - 1, at] = summed(n, slot, [slot | d for d in down[:stage]]).astype(jnp.bfloat16)
            d = down[stage]
            key = (n, way, slot ^ d)
            send(outgoing.at[slot - 1, at], incoming.at[slot - 1, at], down_send, recv_sem.at[NUMBER[key]], peer[d])
        else:
            need(("load", 4), loads[4].wait)
            need(("load", 5), loads[5].wait)
            gradient = summed(n, 0, down) / 16
            old_master, old_momentum = master_in[at], momentum_in[at]
            interp = beta_one * old_momentum + (1.0 - beta_one) * gradient
            direction = interp * lax.rsqrt(interp * interp + softness * softness)
            fresh = old_master - step_size * (direction + decay_rate * old_master)
            weights[y, xh, core, at] = fresh.astype(jnp.bfloat16)
            pass_up(n, 0, up)
            new_master[at] = fresh
            new_momentum[at] = beta_two * old_momentum + (1.0 - beta_two) * gradient

    for sem in (twin_recv, twin_send, pair_send):
        await_bytes(own, sem)
    for sem in (down_send, up_send):
        await_bytes(outgoing, sem)


def put_out(fresh, moved, rounded, new_master, new_momentum, weights, sem):
    copies = [
        pltpu.make_async_copy(fresh, new_master, sem.at[0]),
        pltpu.make_async_copy(moved, new_momentum, sem.at[1]),
    ]
    for n in range(4):
        copies.append(pltpu.make_async_copy(rounded.at[n], weights.at[n], sem.at[2 + n]))
    for copy in copies:
        copy.start()
    for copy in copies:
        copy.wait()


def per_device(grad_parts, master, momentum):
    side, columns = master.shape[1:]
    grad = grad_parts.reshape(4, 2, 2, side, columns)
    outs = (((side, columns), jnp.float32), ((side, columns), jnp.float32), ((4, 2, 2, side, columns), jnp.bfloat16))
    results = pl.pallas_call(
        kernel,
        out_shape=[pltpu.VMEM(*o) for o in outs],
        in_specs=[pl.BlockSpec(memory_space=pltpu.HBM)] * 3,
        out_specs=[pl.BlockSpec(memory_space=pltpu.VMEM)] * 3,
        scratch_shapes=[
            pltpu.VMEM((4, 2, side, columns), jnp.bfloat16),
            pltpu.VMEM((4, 2, side, columns), jnp.bfloat16),
            pltpu.VMEM((4, 2, side, columns), jnp.bfloat16),
            pltpu.VMEM((7, side, columns), jnp.bfloat16),
            pltpu.VMEM((7, side, columns), jnp.bfloat16),
            pltpu.VMEM((side, columns), jnp.float32),
            pltpu.VMEM((side, columns), jnp.float32),
            pltpu.SemaphoreType.DMA((6,)),
            pltpu.SemaphoreType.DMA((SEMAPHORES,)),
            pltpu.SemaphoreType.DMA,
            pltpu.SemaphoreType.DMA,
            pltpu.SemaphoreType.DMA,
            pltpu.SemaphoreType.DMA,
            pltpu.SemaphoreType.DMA,
        ],
        compiler_params=pltpu.CompilerParams(collective_id=0, has_side_effects=True, vmem_limit_bytes=48 * 2**20),
    )(grad, master.reshape(side, columns), momentum.reshape(side, columns))
    new_master, new_momentum, weights = pl.pallas_call(
        put_out,
        out_shape=[jax.ShapeDtypeStruct(*o) for o in outs],
        in_specs=[pl.BlockSpec(memory_space=pltpu.VMEM)] * 3,
        out_specs=[pl.BlockSpec(memory_space=pltpu.HBM)] * 3,
        scratch_shapes=[pltpu.SemaphoreType.DMA((6,))],
        compiler_params=pltpu.CompilerParams(vmem_limit_bytes=2**20),
    )(*[pltpu.with_memory_space_constraint(r, pltpu.VMEM) for r in results])
    return (
        new_master.reshape(1, side, columns),
        new_momentum.reshape(1, side, columns),
        weights.reshape(1, 16 * side, columns),
    )


def solution(mesh):
    return jax.shard_map(
        per_device,
        mesh=mesh,
        in_specs=(P("dp", None, None, "mp"), P(None, "dp", "mp"), P(None, "dp", "mp")),
        out_specs=(P(None, "dp", "mp"), P(None, "dp", "mp"), P(None, None, "mp")),
        check_vma=False,
    )
```

time: 45.4 us -> 44 us (0.969)
  Pallas kernels: 44.7 us -> 43.3 us
    pallas_call x1, Pallas kernels: 42.1 us -> 40.6 us  [per_device(): pl.pallas_call(kernel, out_shape=[pltpu.VMEM(*o) for o in outs], in_specs...]
where the time goes in v3:
time: 44 us; the launch traced here: 43.9 us
  Pallas kernels  43.3 us (98%)
  between operations  0.64 us (1%)
    pallas_call x1, Pallas kernels, per_device(): pl.pallas_call(kernel, out_shape=[pltpu.VMEM(*o) for o in outs], in_specs...  40.6 us
    pallas_call x1, Pallas kernels, per_device(): pl.pallas_call(put_out, out_shape=[jax.ShapeDtypeStruct(*o) for o in outs...  2.62 us

profile of v3, /device:TPU:1, one launch (start us, length us, event | category | flops | bytes accessed | tf_op | source)
XLA Modules:
  0.0 43.9 jit_solution(1835292823575282136)
XLA Ops:
  0.6 40.6 %shard_map.58 = (f32[384,384]{1,0:T(8,128)S(1)}, f32[384,384]{1,0:T(8,128)S(1)}, bf16[4,2,2,384,384]{4,3,2,1,0:T(8,128)(2,1)S(1)}) custom-call(bf16[4,2,2,384,384]{4,3,2,1,0:T(8,128)(2,1)} %bitcast.6, f32[384,384]{1,0:T(8,128)} %bitcast.7, f32[384,384]{1,0:T(8,128)} %bitcast.8), custom_call_target="tpu_custom_call" | custom-call | tf_op jit(solution)/shard_map/pallas_call | solution.py:247
  41.3 2.6 %shard_map.59 = (f32[384,384]{1,0:T(8,128)}, f32[384,384]{1,0:T(8,128)}, bf16[4,2,2,384,384]{4,3,2,1,0:T(8,128)(2,1)}) custom-call(f32[384,384]{1,0:T(8,128)S(1)} %get-tuple-element.9.fresh, f32[384,384]{1,0:T(8,128)S(1)} %get-tuple-element.10.moved, bf16[4,2,2,384,384]{4,3,2,1,0:T(8,128)(2,1)S(1)} %get-tuple-element.11.rounded), custom_call_target="tpu_custom_call" | custom-call | tf_op jit(solution)/shard_map/pallas_call | solution.py:270

commit v4 on v3

--- a/solution.py
+++ b/solution.py
@@ -17,24 +17,26 @@
 A, B, X = 4, 2, 1
 
 PIECES = (
-    (0, 32, (B, A, X), (A, X, B)),
-    (32, 32, (X, A, B), (A, X, B)),
-    (64, 32, (X, A, B), (X, A, B)),
-    (96, 48, (A, X, B), (X, A, B)),
-    (144, 64, (B, A, X), (B, A, X)),
-    (208, 32, (B, A, X), (A, B, X)),
-    (240, 48, (X, A, B), (B, A, X)),
-    (288, 48, (X, B, A), (X, A, B)),
-    (336, 48, (B, A, X), (X, A, B)),
+    (0, 32, (B, A, X), (B, X, A)),
+    (32, 80, (X, A, B), (B, X, A)),
+    (112, 16, (B, A, X), (A, B, X)),
+    (128, 32, (A, X, B), (B, X, A)),
+    (160, 48, (X, B, A), (X, B, A)),
+    (208, 32, (X, A, B), (X, B, A)),
+    (240, 48, (A, B, X), (X, A, B)),
+    (288, 48, (B, A, X), (A, B, X)),
+    (336, 32, (B, A, X), (A, B, X)),
+    (368, 16, (A, B, X), (A, B, X)),
 )
-EARLY = 64
+EARLY = 112
 STEPS = (
-    7, 21, 23, 2, 3, 19, 71, 55, 103, 86, 52, 82, 135, 39, 67, 54, 134, 101, 87, 37,
-    35, 119, 5, 99, 53, 69, 6, 33, 117, 51, 70, 131, 102, 115, 22, 133, 36, 1, 38, 84,
-    65, 118, 83, 98, 66, 85, 130, 49, 113, 68, 129, 50, 4, 100, 81, 116, 20, 17, 114, 34,
-    132, 18, 97, 72, 56, 8, 120, 24, 88, 136, 104, 12, 40, 121, 74, 25, 92, 28, 60, 57,
-    106, 137, 108, 13, 94, 9, 140, 76, 124, 78, 41, 110, 75, 125, 30, 29, 141, 44, 61, 90,
-    93, 45, 123, 127, 43, 59, 31, 14, 79, 15, 107, 139, 111, 63, 95, 143, 47,
+    7, 2, 3, 6, 23, 53, 54, 115, 102, 55, 151, 119, 67, 103, 135, 134, 100, 87, 69, 85,
+    5, 71, 17, 83, 39, 150, 19, 101, 149, 148, 130, 114, 131, 38, 147, 99, 22, 98, 21, 86,
+    1, 52, 133, 35, 146, 70, 37, 36, 51, 145, 132, 65, 118, 4, 34, 117, 18, 97, 49, 84,
+    33, 81, 129, 66, 20, 82, 68, 50, 8, 113, 116, 152, 104, 24, 56, 40, 72, 120, 10, 88,
+    154, 136, 58, 44, 156, 105, 26, 9, 73, 42, 124, 140, 138, 89, 108, 158, 122, 25, 46, 107,
+    57, 74, 14, 45, 59, 75, 11, 109, 126, 27, 62, 77, 142, 90, 91, 47, 111, 159, 93, 141,
+    79, 125, 15, 157, 63, 127, 31, 30, 143, 95,
 )
 
 
@@ -78,16 +80,15 @@
     for at, step in enumerate(STEPS):
         n, slot, way = parse(step)
         halves = () if way == "up" else (0,) if stage_of(PIECES[n][2], slot) == 0 else (0, 1)
-        for key in [(n, way, slot)] + [(n, "pair", half) for half in halves]:
+        for key in [(n, way, slot)] + [(n * (1 - half), "pair", half) for half in halves]:
             first.setdefault(key, at)
         for d, key in messages_of(step):
             sent.setdefault(key, []).append((d, at))
     links = [(d, at, first[key]) for key in sent for d, at in sent[key]]
     number, last = {}, []
-    for n in range(len(PIECES)):
-        for half in range(2):
-            number[n, "pair", half] = len(last)
-            last.append(first[n, "pair", half])
+    for n, half in [(n, 0) for n in range(len(PIECES))] + [(0, 1)]:
+        number[n, "pair", half] = len(last)
+        last.append(first[n, "pair", half])
     for key in sorted(sent, key=lambda k: min(at for _, at in sent[k])):
         fit = [
             (then, i)
@@ -169,7 +170,7 @@
             else:
                 spots = [(y_of[k], slice(None)) for k in ((2, 3), (0, 1))[half]]
             for ty, tx in spots:
-                send(other.at[ty, tx, at], part.at[ty, tx, at], pair_send, recv_sem.at[NUMBER[n, "pair", half]], twin)
+                send(other.at[ty, tx, at], part.at[ty, tx, at], pair_send, recv_sem.at[NUMBER[n * (1 - half), "pair", half]], twin)
 
     def pass_up(n, slot, along):
         ty, tx = tile_of(slot)
@@ -201,8 +202,9 @@
         load = 1 if first < EARLY else 3
         need(("load", load), loads[load].wait)
         stage = stage_of(down, slot)
-        for half in range(2 if stage else 1):
-            need(("part", n, half), lambda: await_bytes(part.at[:, 0, at], recv_sem.at[NUMBER[n, "pair", half]]))
+        need(("part", n), lambda: await_bytes(part.at[:, 0, at], recv_sem.at[NUMBER[n, "pair", 0]]))
+        if stage:
+            need("part", lambda: await_bytes(part.at[:, 0], recv_sem.at[NUMBER[0, "pair", 1]]))
         if slot:
             outgoing[slot - 1, at] = summed(n, slot, [slot | d for d in down[:stage]]).astype(jnp.bfloat16)
             d = down[stage]

time: 44 us -> 43.5 us (0.989)
  Pallas kernels: 43.3 us -> 42.8 us
    pallas_call x1, Pallas kernels: 40.6 us -> 40.2 us  [per_device(): pl.pallas_call(kernel, out_shape=[pltpu.VMEM(*o) for o in outs], in_specs...]
where the time goes in v4:
time: 43.5 us; the launch traced here: 43.4 us
  Pallas kernels  42.8 us (98%)
  between operations  0.64 us (1%)
    pallas_call x1, Pallas kernels, per_device(): pl.pallas_call(kernel, out_shape=[pltpu.VMEM(*o) for o in outs], in_specs...  40.2 us
    pallas_call x1, Pallas kernels, per_device(): pl.pallas_call(put_out, out_shape=[jax.ShapeDtypeStruct(*o) for o in outs...  2.62 us

profile of v4, /device:TPU:1, one launch (start us, length us, event | category | flops | bytes accessed | tf_op | source)
XLA Modules:
  0.0 43.4 jit_solution(6280265226243731518)
XLA Ops:
  0.6 40.2 %shard_map.58 = (f32[384,384]{1,0:T(8,128)S(1)}, f32[384,384]{1,0:T(8,128)S(1)}, bf16[4,2,2,384,384]{4,3,2,1,0:T(8,128)(2,1)S(1)}) custom-call(bf16[4,2,2,384,384]{4,3,2,1,0:T(8,128)(2,1)} %bitcast.6, f32[384,384]{1,0:T(8,128)} %bitcast.7, f32[384,384]{1,0:T(8,128)} %bitcast.8), custom_call_target="tpu_custom_call" | custom-call | tf_op jit(solution)/shard_map/pallas_call | solution.py:249
  40.8 2.6 %shard_map.59 = (f32[384,384]{1,0:T(8,128)}, f32[384,384]{1,0:T(8,128)}, bf16[4,2,2,384,384]{4,3,2,1,0:T(8,128)(2,1)}) custom-call(f32[384,384]{1,0:T(8,128)S(1)} %get-tuple-element.9.fresh, f32[384,384]{1,0:T(8,128)S(1)} %get-tuple-element.10.moved, bf16[4,2,2,384,384]{4,3,2,1,0:T(8,128)(2,1)S(1)} %get-tuple-element.11.rounded), custom_call_target="tpu_custom_call" | custom-call | tf_op jit(solution)/shard_map/pallas_call | solution.py:272

commit v5 on v4

--- a/solution.py
+++ b/solution.py
@@ -147,7 +147,7 @@
             loads.append(pltpu.make_async_copy(grad.at[:, :, of, at], to.at[:, :, at], load_sem.at[len(loads)]))
     loads.append(pltpu.make_async_copy(master, master_in, load_sem.at[4]))
     loads.append(pltpu.make_async_copy(momentum, momentum_in, load_sem.at[5]))
-    for load in loads:
+    for load in loads[:4]:
         load.start()
     there = set()
 
@@ -171,6 +171,9 @@
                 spots = [(y_of[k], slice(None)) for k in ((2, 3), (0, 1))[half]]
             for ty, tx in spots:
                 send(other.at[ty, tx, at], part.at[ty, tx, at], pair_send, recv_sem.at[NUMBER[n * (1 - half), "pair", half]], twin)
+
+    for load in loads[4:]:
+        load.start()
 
     def pass_up(n, slot, along):
         ty, tx = tile_of(slot)

time: 43.5 us -> 43.5 us (level)
  no operation moved by 1% of the time
where the time goes in v5:
time: 43.5 us; the launch traced here: 43.4 us
  Pallas kernels  42.8 us (98%)
  between operations  0.64 us (1%)
    pallas_call x1, Pallas kernels, per_device(): pl.pallas_call(kernel, out_shape=[pltpu.VMEM(*o) for o in outs], in_specs...  40.2 us
    pallas_call x1, Pallas kernels, per_device(): pl.pallas_call(put_out, out_shape=[jax.ShapeDtypeStruct(*o) for o in outs...  2.62 us

profile of v5, /device:TPU:1, one launch (start us, length us, event | category | flops | bytes accessed | tf_op | source)
XLA Modules:
  0.0 43.4 jit_solution(17762153050583322279)
XLA Ops:
  0.6 40.2 %shard_map.58 = (f32[384,384]{1,0:T(8,128)S(1)}, f32[384,384]{1,0:T(8,128)S(1)}, bf16[4,2,2,384,384]{4,3,2,1,0:T(8,128)(2,1)S(1)}) custom-call(bf16[4,2,2,384,384]{4,3,2,1,0:T(8,128)(2,1)} %bitcast.6, f32[384,384]{1,0:T(8,128)} %bitcast.7, f32[384,384]{1,0:T(8,128)} %bitcast.8), custom_call_target="tpu_custom_call" | custom-call | tf_op jit(solution)/shard_map/pallas_call | solution.py:252
  40.8 2.6 %shard_map.59 = (f32[384,384]{1,0:T(8,128)}, f32[384,384]{1,0:T(8,128)}, bf16[4,2,2,384,384]{4,3,2,1,0:T(8,128)(2,1)}) custom-call(f32[384,384]{1,0:T(8,128)S(1)} %get-tuple-element.9.fresh, f32[384,384]{1,0:T(8,128)S(1)} %get-tuple-element.10.moved, bf16[4,2,2,384,384]{4,3,2,1,0:T(8,128)(2,1)S(1)} %get-tuple-element.11.rounded), custom_call_target="tpu_custom_call" | custom-call | tf_op jit(solution)/shard_map/pallas_call | solution.py:275
